TPU v7x, 32 devices: a whole 2x2x4 slice. The times are simulated.
32 devices in a mesh: space: 8 (over z, y), tm: 4 (over x, core).
Axes of the slice: x: 2, y: 2, z: 4, core: 2. Of those that a mesh axis runs over, the one named last changes fastest.
Arguments:
- precip: float32 [512, 48, 2048], P('tm', 'space'), may hold values from 0.0001 to 0.01
Outputs:
- totals: float32 [48, 2048, 512], P(None, 'space', 'tm')
All inputs are finite; a program needn't handle non-finite values.
Results may differ from a plain program's by a relative error of at most 0.00005.
Values sent between devices are 32-bit elements; how exact they have to be, the bound alone decides.
A program may use at most 64 MiB of HBM per device.

v0:
```python
import jax
import jax.numpy as jnp
from jax import lax
from jax.sharding import PartitionSpec as P


def entering(part, axis, combine, identity):
    place = lax.axis_index(axis)
    gathered = lax.all_gather(part, axis)
    state = jnp.zeros_like(part) + jnp.asarray(identity, part.dtype)

    def one(turn, state):
        return combine(state, lax.dynamic_index_in_dim(gathered, turn, 0, False))

    return lax.fori_loop(0, place, one, state)


def rechunk(source):
    return lax.all_to_all(source, "space", split_axis=2, concat_axis=1, tiled=True)


def add_terms(earlier_part, later_part):
    return earlier_part + later_part


def day_prefix(pixel_major, upper_ones):
    lat_rows, lon_cols, day_count = pixel_major.shape
    flat_rows = pixel_major.reshape(lat_rows * lon_cols, day_count)
    summed = jnp.dot(
        flat_rows, upper_ones, precision=lax.Precision.HIGHEST, preferred_element_type=jnp.float32
    )
    return summed.reshape(lat_rows, lon_cols, day_count)


def per_device(precip):
    day_count = precip.shape[0]
    position = lax.broadcasted_iota(jnp.int32, (day_count, day_count), 0)
    later_pos = lax.broadcasted_iota(jnp.int32, (day_count, day_count), 1)
    upper_ones = (position <= later_pos).astype(jnp.float32)
    pixel_major = jnp.transpose(rechunk(precip), (1, 2, 0))
    running = day_prefix(pixel_major, upper_ones)
    last_day = running[:, :, -1]
    carried = entering(last_day, "tm", add_terms, jnp.zeros_like(last_day))
    return running + carried[:, :, None]


def solution(mesh):
    return jax.shard_map(
        per_device,
        mesh=mesh,
        in_specs=(P("tm", "space", None),),
        out_specs=P(None, "space", "tm"),
        check_vma=False,
    )
```

profile of v0, /device:TPU:8, one launch (start us, length us, event | category | flops | bytes accessed | tf_op | source)
XLA Modules:
  0.0 228.1 jit_solution(16729160938471448487)
XLA Ops:
  0.0 8.4 %copy.8 = f32[128,6,2048]{0,1,2:T(8,128)} copy(f32[128,6,2048]{2,0,1:T(8,128)} %param.3) | data formatting | bytes 12582912 | tf_op args[0]
  8.4 6.3 %all-to-all-start = ((f32[128,6,2048]{0,1,2:T(8,128)}), f32[128,6,2048]{0,1,2:T(8,128)}, u32[]{:S(2)}, u32[]{:S(2)}) async-start(f32[128,6,2048]{0,1,2:T(8,128)} %copy.8), calls=%async_computation | async-start | bytes 16777216 | tf_op jit(solution)/shard_map/all_to_all | solution.py:19
  14.7 180.6 %all-to-all-done = f32[128,6,2048]{0,1,2:T(8,128)} async-done(((f32[128,6,2048]{0,1,2:T(8,128)}), f32[128,6,2048]{0,1,2:T(8,128)}, u32[]{:S(2)}, u32[]{:S(2)}) %all-to-all-start) | async-done | bytes 6291488 | tf_op jit(solution)/shard_map/all_to_all | solution.py:19
  195.3 4.5 %copy.14 = f32[128,8,6,256]{0,3,2,1:T(8,128)S(1)} copy(f32[128,8,6,256]{0,2,3,1:T(8,128)} %bitcast.3) | data formatting | bytes 12582912 | tf_op jit(solution)/shard_map/transpose | solution.py:40
  199.8 3.3 %fusion.1 = f32[128,12288]{1,0:T(8,128)S(1)} fusion(f32[12288,128]{1,0:T(8,128)S(1)} %bitcast.21), kind=kOutput, calls=%fused_computation.4 | convolution fusion | flops 2415951872 | bytes 12582912 | tf_op jit(solution)/shard_map/dot_general | solution.py:29
  203.1 4.7 %copy.15 = f32[16,8,48,256]{3,2,1,0:T(8,128)} copy(f32[16,8,48,256]{3,1,2,0:T(8,128)S(1)} %bitcast.22) | data formatting | bytes 12582912
  207.7 6.7 %copy.12 = f32[48,256,128]{2,1,0:T(8,128)} copy(f32[48,256,128]{1,0,2:T(8,128)} %bitcast.19) | data formatting | bytes 12582912 | tf_op jit(solution)/shard_map/reshape | solution.py:32
  214.4 0.8 slice.4
  215.2 5.6 %all-gather = f32[192,256,1]{1,0,2:T(8,128)S(1)} all-gather(f32[48,256,1]{1,0,2:T(8,128)S(1)} %slice.4), channel_id=2, replica_groups=mesh['space'=8,'tm'=4] {'tm'}, dimensions={0}, use_global_device_ids=true | all-gather | bytes 245760 | tf_op jit(solution)/shard_map/all_gather | solution.py:9
  220.8 7.2 %broadcast_add_fusion = f32[48,256,128]{2,1,0:T(8,128)} fusion(f32[48,256,128]{2,1,0:T(8,128)} %copy.12, f32[48,256]{1,0:T(8,128)S(1)} %get-tuple-element.28), kind=kLoop, calls=%fused_computation.1 | loop fusion | flops 1572864 | bytes 12632064 | tf_op jit(solution)/shard_map/add | solution.py:44
  (2 shorter events, 0.0 us)
Async XLA Ops:
  8.4 186.9 %all-to-all-start = ((f32[128,6,2048]{0,1,2:T(8,128)}), f32[128,6,2048]{0,1,2:T(8,128)}, u32[]{:S(2)}, u32[]{:S(2)}) async-start(f32[128,6,2048]{0,1,2:T(8,128)} %copy.8), calls=%async_computation | async-start | bytes 16777216 | tf_op jit(solution)/shard_map/all_to_all | solution.py:19
where the time goes:
time: 232 us; the launch traced here: 228 us
  waiting for transfers between devices  181 us (78%)
  local copies, waits for them, and re-layouts  25 us (11%)
  other arithmetic  7.24 us (3%)
  starting transfers between devices  6.28 us (3%)
  blocking collectives  5.58 us (2%)
  matrix products  3.3 us (1%)
    all_to_all x1, waiting for transfers between devices, rechunk(): lax.all_to_all(source, 'space', split_axis=2, concat_axis=1, tiled=True)  181 us
    unnamed x2, local copies, waits for them, and re-layouts  13.1 us
    add x1, other arithmetic, per_device(): return running + carried[:, :, None]  7.24 us
    reshape x1, local copies, waits for them, and re-layouts, day_prefix(): return summed.reshape(lat_rows, lon_cols, day_count)  6.69 us
    all_to_all x1, starting transfers between devices, rechunk(): lax.all_to_all(source, 'space', split_axis=2, concat_axis=1, tiled=True)  6.28 us
    all_gather x1, blocking collectives, entering(): gathered = lax.all_gather(part, axis)  5.58 us
  transfers between devices with their start and end apart: 1, of which 1 were waited for; matrix products, arithmetic and copies ran while one was open for 0% of the time, Pallas kernels for 0%

commit v1 on v0

v1 whole, which is shorter than its diff:
```python
import functools

import jax
import jax.numpy as jnp
from jax import lax
from jax.experimental import pallas as pl
from jax.experimental.pallas import tpu as pltpu
from jax.sharding import PartitionSpec as P

MESH = pl.DeviceIdType.MESH
HEAD = 8
CHUNKS = 2
FIRST = 3


def flip(place, mask):
    value, bit = 0, 1
    while bit <= mask:
        value = value + ((place // bit + mask // bit) % 2) * bit
        bit *= 2
    return value + (place // bit) * bit


def peer_at(place, step, size):
    if size & (size - 1) == 0:
        return flip(place, step)
    return lax.rem(place + step, size)


def source_at(place, step, size):
    if size & (size - 1) == 0:
        return flip(place, step)
    return lax.rem(place + size - step, size)


def kernel(spaces, times, chunks, x_ref, out_ref, held, arrived, tot, tots, ones,
           load_sem, main_send, main_recv, head_send, head_recv, tot_send, tot_recv):
    lat, days, lon = x_ref.shape
    block = lon // spaces
    part = lat // chunks
    me = lax.axis_index("space")
    when = lax.axis_index("tm")

    loads = [pltpu.make_async_copy(x_ref.at[a], held.at[a], load_sem.at[a]) for a in range(lat)]
    barrier = pltpu.get_barrier_semaphore()
    for step in range(1, spaces):
        pl.semaphore_signal(barrier, inc=1, device_id={"space": peer_at(me, step, spaces)}, device_id_type=MESH)
    for step in range(1, times):
        pl.semaphore_signal(barrier, inc=1, device_id={"tm": lax.rem(when + step, times)}, device_id_type=MESH)
    for load in loads:
        load.start()
    pl.semaphore_wait(barrier, spaces - 1 + times - 1)

    def columns(step):
        peer = peer_at(me, step, spaces)
        return peer, pl.ds(pl.multiple_of(peer * block, block), block)

    def main(step, c):
        peer, cols = columns(step)
        return pltpu.make_async_remote_copy(
            src_ref=x_ref.at[pl.ds(c * part, part), pl.ds(HEAD, days - HEAD), cols],
            dst_ref=arrived.at[step - 1, pl.ds(c * part, part), pl.ds(HEAD, days - HEAD)],
            send_sem=main_send.at[step - 1, c],
            recv_sem=main_recv.at[step - 1, c],
            device_id={"space": peer},
            device_id_type=MESH,
        )

    def head(step):
        peer, cols = columns(step)
        return pltpu.make_async_remote_copy(
            src_ref=held.at[:, pl.ds(0, HEAD), cols],
            dst_ref=arrived.at[step - 1, :, pl.ds(0, HEAD)],
            send_sem=head_send.at[step - 1],
            recv_sem=head_recv.at[step - 1],
            device_id={"space": peer},
            device_id_type=MESH,
        )

    def total(step):
        return pltpu.make_async_remote_copy(
            src_ref=tot,
            dst_ref=tots.at[step - 1],
            send_sem=tot_send.at[step - 1],
            recv_sem=tot_recv.at[step - 1],
            device_id={"tm": lax.rem(when + step, times)},
            device_id_type=MESH,
        )

    first = min(FIRST, spaces - 1)
    for step in range(1, first + 1):
        for c in range(chunks):
            main(step, c).start()

    for a in range(lat):
        loads[a].wait()
        tot[a] = jnp.sum(held[a], axis=0, keepdims=True)
    position = lax.broadcasted_iota(jnp.int32, (days, days), 0)
    later = lax.broadcasted_iota(jnp.int32, (days, days), 1)
    ones[...] = (position <= later).astype(jnp.float32)
    for step in range(1, times):
        total(step).start()
    for step in range(1, times):
        total(step).wait_recv()
    for a in range(lat):
        carry = jnp.zeros((1, lon), jnp.float32)
        for step in range(1, times):
            earlier = jnp.where(when >= step, 1.0, 0.0)
            carry = carry + tots[step - 1, a] * earlier
        held[a, 0:1, :] = held[a, 0:1, :] + carry

    def prefix(x):
        return lax.dot_general(
            x.T, ones[...], (((1,), (0,)), ((), ())),
            precision=lax.Precision.HIGHEST, preferred_element_type=jnp.float32,
        )

    for step in range(1, spaces):
        head(step).start()
    for step in range(first + 1, spaces):
        for c in range(chunks):
            main(step, c).start()

    mine = pl.ds(pl.multiple_of(me * block, block), block)

    @pl.loop(0, lat)
    def _(a):
        out_ref[me * lat + a] = prefix(held[a, :, mine])

    for step in range(1, spaces):
        source = source_at(me, step, spaces)
        head(step).wait_recv()
        for c in range(chunks):
            main(step, c).wait_recv()

            @pl.loop(c * part, (c + 1) * part)
            def _(a):
                out_ref[source * lat + a] = prefix(arrived[step - 1, a])

    for step in range(1, times):
        total(step).wait_send()
    for step in range(1, spaces):
        head(step).wait_send()
        for c in range(chunks):
            main(step, c).wait_send()


def direct(spaces, times, precip):
    days, lat, lon = precip.shape
    chunks = CHUNKS if lat % CHUNKS == 0 else 1
    block = lon // spaces
    rows = jnp.transpose(precip, (1, 0, 2))
    dma = pltpu.SemaphoreType.DMA
    return pl.pallas_call(
        functools.partial(kernel, spaces, times, chunks),
        out_shape=jax.ShapeDtypeStruct((lat * spaces, block, days), jnp.float32),
        in_specs=[pl.BlockSpec(memory_space=pltpu.HBM)],
        out_specs=pl.BlockSpec(memory_space=pltpu.VMEM),
        scratch_shapes=[
            pltpu.VMEM((lat, days, lon), jnp.float32),
            pltpu.VMEM((spaces - 1, lat, days, block), jnp.float32),
            pltpu.VMEM((lat, 1, lon), jnp.float32),
            pltpu.VMEM((times - 1, lat, 1, lon), jnp.float32),
            pltpu.VMEM((days, days), jnp.float32),
            dma((lat,)),
            dma((spaces - 1, chunks)),
            dma((spaces - 1, chunks)),
            dma((spaces - 1,)),
            dma((spaces - 1,)),
            dma((times - 1,)),
            dma((times - 1,)),
        ],
        compiler_params=pltpu.CompilerParams(
            collective_id=0, has_side_effects=True, vmem_limit_bytes=55 * 2**20
        ),
        name="rechunk",
    )(rows)


def plain(precip):
    days = precip.shape[0]
    position = lax.broadcasted_iota(jnp.int32, (days, days), 0)
    later = lax.broadcasted_iota(jnp.int32, (days, days), 1)
    ones = (position <= later).astype(jnp.float32)
    source = lax.all_to_all(precip, "space", split_axis=2, concat_axis=1, tiled=True)
    pixel_major = jnp.transpose(source, (1, 2, 0))
    running = jnp.dot(
        pixel_major, ones, precision=lax.Precision.HIGHEST, preferred_element_type=jnp.float32
    )
    last = lax.all_gather(running[:, :, -1], "tm")
    place = lax.broadcasted_iota(jnp.int32, last.shape, 0)
    carried = jnp.sum(jnp.where(place < lax.axis_index("tm"), last, 0.0), axis=0)
    return running + carried[:, :, None]


def solution(mesh):
    spaces, times = mesh.shape["space"], mesh.shape["tm"]

    def per_device(precip):
        days, _, lon = precip.shape
        tiled = lon % (spaces * 128) == 0 and days % 128 == 0
        if tiled and spaces > 1 and times > 1:
            return direct(spaces, times, precip)
        return plain(precip)

    return jax.shard_map(
        per_device,
        mesh=mesh,
        in_specs=(P("tm", "space", None),),
        out_specs=P(None, "space", "tm"),
        check_vma=False,
    )
```

time: 232 us -> 156 us (0.67); the launches traced: 228 us -> 156 us
  waiting for transfers between devices: 181 us -> 0 us
  Pallas kernels: 0 us -> 150 us
  local copies, waits for them, and re-layouts: 25 us -> 6.2 us
  other arithmetic: 7.24 us -> 0 us
  starting transfers between devices: 6.28 us -> 0 us
  blocking collectives: 5.58 us -> 0 us
  matrix products: 3.3 us -> 0 us
    all_to_all x1 -> x0, waiting for transfers between devices: 181 us -> none  [rechunk(): lax.all_to_all(source, 'space', split_axis=2, concat_axis=1, tiled=True)]
    pallas_call x0 -> x1, Pallas kernels: none -> 150 us  [direct(): pl.pallas_call(functools.partial(kernel, spaces, times, chunks), out_shap...]
    add x1 -> x0, other arithmetic: 7.24 us -> none  [per_device(): return running + carried[:, :, None]]
    unnamed x2 -> x1, local copies, waits for them, and re-layouts: 13.1 us -> 6.2 us
    reshape x1 -> x0, local copies, waits for them, and re-layouts: 6.69 us -> none  [day_prefix(): return summed.reshape(lat_rows, lon_cols, day_count)]
    all_to_all x1 -> x0, starting transfers between devices: 6.28 us -> none  [rechunk(): lax.all_to_all(source, 'space', split_axis=2, concat_axis=1, tiled=True)]
    all_gather x1 -> x0, blocking collectives: 5.58 us -> none  [entering(): gathered = lax.all_gather(part, axis)]
    transpose x1 -> x0, local copies, waits for them, and re-layouts: 4.49 us -> none  [per_device(): pixel_major = jnp.transpose(rechunk(precip), (1, 2, 0))]
  transfers between devices with their start and end apart: 1 -> 0, of which waited for: 1 -> 0; matrix products, arithmetic and copies ran while one was open for 0% -> 0% of each run, Pallas kernels for 0% -> 0%
where the time goes in v1:
time: 156 us
  Pallas kernels  150 us (96%)
  local copies, waits for them, and re-layouts  6.2 us (4%)
    pallas_call x1, Pallas kernels, direct(): pl.pallas_call(functools.partial(kernel, spaces, times, chunks), out_shap...  150 us
    unnamed x1, local copies, waits for them, and re-layouts  6.2 us

profile of v1, /device:TPU:8, one launch (start us, length us, event | category | flops | bytes accessed | tf_op | source)
XLA Modules:
  0.0 156.0 jit_solution(10460394098978169957)
XLA Ops:
  0.0 149.8 %rechunk.1 = f32[48,256,128]{2,1,0:T(8,128)} custom-call(f32[6,128,2048]{2,1,0:T(8,128)} %bitcast.1), custom_call_target="tpu_custom_call" | custom-call | tf_op jit(solution)/shard_map/rechunk/pallas_call | solution.py:154
  149.8 6.2 %copy.3 = f32[48,256,128]{2,1,0:T(8,128)} copy(f32[48,256,128]{2,1,0:T(8,128)} %rechunk.1) | data formatting | bytes 12582912

commit v2 on v1

--- a/solution.py
+++ b/solution.py
@@ -13,23 +13,30 @@
 FIRST = 3
 
 
-def flip(place, mask):
+def turns_of(spaces):
+    near = list(range(1, spaces))
+    if spaces & (spaces - 1) or spaces < 4:
+        return near, near
+    return near, [step ^ 1 for step in near[1:]] + [1]
+
+
+def flip(place, mask, size):
     value, bit = 0, 1
-    while bit <= mask:
+    while bit < size:
         value = value + ((place // bit + mask // bit) % 2) * bit
         bit *= 2
-    return value + (place // bit) * bit
+    return value
 
 
 def peer_at(place, step, size):
     if size & (size - 1) == 0:
-        return flip(place, step)
+        return flip(place, step, size)
     return lax.rem(place + step, size)
 
 
 def source_at(place, step, size):
     if size & (size - 1) == 0:
-        return flip(place, step)
+        return flip(place, step, size)
     return lax.rem(place + size - step, size)
 
 
@@ -88,7 +95,9 @@
         )
 
     first = min(FIRST, spaces - 1)
-    for step in range(1, first + 1):
+    even, odd = turns_of(spaces)
+    turns = [a if a == b else jnp.where(when % 2 == 0, a, b) for a, b in zip(even, odd)]
+    for step in turns[:first]:
         for c in range(chunks):
             main(step, c).start()
 
@@ -115,9 +124,9 @@
             precision=lax.Precision.HIGHEST, preferred_element_type=jnp.float32,
         )
 
-    for step in range(1, spaces):
+    for step in turns:
         head(step).start()
-    for step in range(first + 1, spaces):
+    for step in turns[first:]:
         for c in range(chunks):
             main(step, c).start()
 
@@ -127,7 +136,7 @@
     def _(a):
         out_ref[me * lat + a] = prefix(held[a, :, mine])
 
-    for step in range(1, spaces):
+    for step in turns:
         source = source_at(me, step, spaces)
         head(step).wait_recv()
         for c in range(chunks):
@@ -171,7 +180,7 @@
             dma((times - 1,)),
         ],
         compiler_params=pltpu.CompilerParams(
-            collective_id=0, has_side_effects=True, vmem_limit_bytes=55 * 2**20
+            collective_id=0, has_side_effects=True, vmem_limit_bytes=46 * 2**20
         ),
         name="rechunk",
     )(rows)

time: 156 us -> 144 us (0.923)
  Pallas kernels: 150 us -> 142 us
  local copies, waits for them, and re-layouts: 6.2 us -> 2.71 us
    pallas_call x1, Pallas kernels: 150 us -> 142 us  [direct(): pl.pallas_call(functools.partial(kernel, spaces, times, chunks), out_shap...]
    unnamed x1, local copies, waits for them, and re-layouts: 6.2 us -> 2.71 us
where the time goes in v2:
time: 144 us
  Pallas kernels  142 us (99%)
  local copies, waits for them, and re-layouts  2.71 us (2%)
    pallas_call x1, Pallas kernels, direct(): pl.pallas_call(functools.partial(kernel, spaces, times, chunks), out_shap...  142 us

profile of v2, /device:TPU:8, one launch (start us, length us, event | category | flops | bytes accessed | tf_op | source)
XLA Modules:
  0.0 144.3 jit_solution(5779856882293379766)
XLA Ops:
  0.0 141.6 %rechunk.1 = f32[48,256,128]{2,1,0:T(8,128)S(1)} custom-call(f32[6,128,2048]{2,1,0:T(8,128)} %bitcast.1), custom_call_target="tpu_custom_call" | custom-call | tf_op jit(solution)/shard_map/rechunk/pallas_call | solution.py:163
  141.6 2.7 %copy.3 = f32[48,256,128]{2,1,0:T(8,128)} copy(f32[48,256,128]{2,1,0:T(8,128)S(1)} %rechunk.1) | data formatting | bytes 12582912
